TPU v7x, 32 devices: a whole 2x2x4 slice. The times are simulated.
32 devices in a mesh: pool: 4 (over y, core), ga: 8 (over z, x).
Axes of the slice: x: 2, y: 2, z: 4, core: 2. Of those that a mesh axis runs over, the one named last changes fastest.
Arguments:
- coefficients: bfloat16 [4, 256, 2, 256, 128], P('pool', 'ga'), may hold values from -6 to 6
- stick_count: int32 [4, 8], P('pool', 'ga'), may hold values from 28 to 32, as said below
- dest_device: int32 [4, 256], P('pool', 'ga'), may hold values from -1 to 7, as said below
- dest_slot: int32 [4, 256], P('pool', 'ga'), may hold values from -1 to 31, as said below
- source_stick: int32 [4, 256], P('pool', 'ga'), may hold values from -1 to 255, as said below
Outputs:
- margins: float32 [4, 2, 256, 256], P('pool', None, 'ga')
Inputs may be any that keep to these rules, and one draw needn't show every extreme that they name: Every k-point has a device whose 32 slots are all live; a device's live sticks are its first stick_count slots. `dest_device`: -1 exactly for sticks that land nowhere (among them all sticks that are not live); no device sends more than 8 of its sticks to one device, and some pair of devices reaches 8 for every k-point. `dest_slot`: -1 where dest_device is -1; the slots named are live slots of the layout of k-point q-1, no slot named twice. `source_stick`: the exact inverse of dest_device and dest_slot: a slot names a stick exactly when that stick names the slot, else -1.
All inputs are finite; a program needn't handle non-finite values.
Results may differ from a plain program's by a relative error of at most 0.0003.
Values may be sent and summed in bfloat16 or wider, within the bound.
A program may use at most 64 MiB of HBM per device.

v0:
```python
import functools

import jax
import jax.numpy as jnp
from jax import lax
from jax.experimental import pallas as pl
from jax.experimental.pallas import tpu as pltpu
from jax.sharding import PartitionSpec as P

MESH = pl.DeviceIdType.MESH
CHUNKS = 8
WINDOW = 2


def kernel(
    scale, coef, count, source, out,
    stage, send, mine, theirs, ket, acc, rs, near_map, far_map, slot_map,
    load_sem, own_sem, send_sem, recv_sem, fsend_sem, frecv_sem,
    map_send, map_recv, fmap_send, fmap_recv, map_sem, rs_send, rs_recv,
):
    groups, pools = lax.axis_size("ga"), lax.axis_size("pool")
    me, pool = lax.axis_index("ga"), lax.axis_index("pool")
    prev, succ = lax.rem(pool + pools - 1, pools), lax.rem(pool + 1, pools)
    slots, _, bands, waves = stage.shape
    width = waves // groups
    depth = 2 * width
    part = slots // CHUNKS
    half = bands // 2
    rows = bands // groups

    def load(c):
        span = pl.ds(c * part, part)
        return pltpu.make_async_copy(coef.at[0, span], stage.at[span], load_sem.at[c])

    def own(c):
        return pltpu.make_async_copy(
            send.at[me, pl.ds(c * part, part)],
            mine.at[pl.ds(me * slots + c * part, part)],
            own_sem.at[c],
        )

    def exchange(c, r):
        dest = lax.rem(me + r, groups)
        return pltpu.make_async_remote_copy(
            src_ref=send.at[dest, pl.ds(c * part, part)],
            dst_ref=mine.at[pl.ds(me * slots + c * part, part)],
            send_sem=send_sem.at[c, r],
            recv_sem=recv_sem.at[c, r],
            device_id={"ga": dest},
            device_id_type=MESH,
        )

    def forward(c, r):
        origin = lax.rem(me + groups - r, groups)
        span = pl.ds(origin * slots + c * part, part)
        return pltpu.make_async_remote_copy(
            src_ref=mine.at[span],
            dst_ref=theirs.at[span],
            send_sem=fsend_sem.at[c, r],
            recv_sem=frecv_sem.at[c, r],
            device_id={"pool": prev},
            device_id_type=MESH,
        )

    def map_copy(r):
        dest = lax.rem(me + r, groups)
        return pltpu.make_async_remote_copy(
            src_ref=source,
            dst_ref=near_map.at[me],
            send_sem=map_send.at[r],
            recv_sem=map_recv.at[r],
            device_id={"ga": dest},
            device_id_type=MESH,
        )

    def map_forward():
        return pltpu.make_async_remote_copy(
            src_ref=near_map,
            dst_ref=far_map,
            send_sem=fmap_send,
            recv_sem=fmap_recv,
            device_id={"pool": prev},
            device_id_type=MESH,
        )

    for c in range(CHUNKS):
        load(c).start()
    own_map = pltpu.make_async_copy(source, near_map.at[me], map_sem)
    own_map.start()

    barrier = pltpu.get_barrier_semaphore()
    for r in range(1, groups):
        pl.semaphore_signal(
            barrier, inc=1, device_id={"ga": lax.rem(me + r, groups)}, device_id_type=MESH
        )
    for other in (prev, succ):
        pl.semaphore_signal(barrier, inc=1, device_id={"pool": other}, device_id_type=MESH)

    def transposed(c):
        load(c).wait()
        for s in range(part):
            slot = c * part + s
            live = slot < count[0, 0]
            for k in range(2):
                block = stage[slot, k]
                block = jnp.where(live, block, jnp.zeros_like(block)).T
                send[:, slot, k * width:(k + 1) * width, :] = block.reshape(groups, width, bands)

    order = [groups // 2] + [r for d in range(1, groups // 2) for r in (groups // 2 - d, groups // 2 + d)]
    order = order[: groups - 1]

    def send_chunk(c):
        for r in order:
            exchange(c, r).start()
        own(c).start()

    def pass_on(c):
        own(c).wait()
        forward(c, 0).start()
        for r in order[::-1]:
            exchange(c, r).wait_recv()
            forward(c, r).start()

    def feed(c, carry):
        transposed(c)
        pass_on(c - WINDOW)
        send_chunk(c)
        return carry

    def finish(c, carry):
        pass_on(c)
        return carry

    transposed(0)
    pl.semaphore_wait(barrier, groups + 1)
    send_chunk(0)
    for c in range(1, WINDOW):
        transposed(c)
    own_map.wait()
    for r in range(1, groups):
        map_copy(r).start()
    for c in range(1, WINDOW):
        send_chunk(c)
    acc[...] = jnp.zeros_like(acc)
    lax.fori_loop(WINDOW, CHUNKS, feed, 0)
    for r in range(1, groups):
        map_copy(r).wait()
    map_forward().start()
    lax.fori_loop(CHUNKS - WINDOW, CHUNKS, finish, 0)
    map_forward().wait()
    to_scalar = pltpu.make_async_copy(far_map, slot_map, map_sem)
    to_scalar.start()
    to_scalar.wait()

    def arrived(c, carry):
        for r in range(groups):
            forward(c, r).wait_recv()
        return carry

    lax.fori_loop(0, CHUNKS, arrived, 0)

    near_half = me // (groups // 2)
    far_half = 1 - near_half

    def gather(b):
        for s in range(slots):
            index = slot_map[b, 0, s]
            block = theirs[jnp.maximum(index, 0)]
            block = jnp.where(index >= 0, block, jnp.zeros_like(block))
            span = pl.ds((b * slots + s) * depth, depth)
            ket[span, 0:bands] = block
            ket[span, bands:2 * bands] = jnp.concatenate([block[width:], -block[:width]], axis=0)

    def product(b, side):
        columns = pl.ds(pl.multiple_of(side * half, half), half)
        bra = mine[pl.ds(b * slots, slots), :, columns].reshape(slots * depth, half)
        other = ket[pl.ds(b * slots * depth, slots * depth), :]
        value = lax.dot_general(
            bra, other, (((0,), (0,)), ((), ())), preferred_element_type=jnp.float32
        )
        span = pl.ds(side * half, half)
        acc[span, :] += value

    def far_step(b, carry):
        gather(b)
        product(b, far_half)
        return carry

    lax.fori_loop(0, groups, far_step, 0)

    def piece(dest):
        return pltpu.make_async_remote_copy(
            src_ref=acc.at[pl.ds(dest * rows, rows)],
            dst_ref=rs.at[me],
            send_sem=rs_send.at[dest],
            recv_sem=rs_recv.at[me],
            device_id={"ga": dest},
            device_id_type=MESH,
        )

    def landed(origin):
        return pltpu.make_async_remote_copy(
            src_ref=acc.at[pl.ds(origin * rows, rows)],
            dst_ref=rs.at[origin],
            send_sem=rs_send.at[origin],
            recv_sem=rs_recv.at[origin],
            device_id={"ga": origin},
            device_id_type=MESH,
        )

    product(0, near_half)
    mates = groups // 2
    for j in range(mates):
        piece(far_half * mates + lax.rem(me + j, mates)).start()

    def near_step(b, carry):
        product(b, near_half)
        return carry

    lax.fori_loop(1, groups, near_step, 0)
    total = acc[pl.ds(me * rows, rows), :]
    rs[pl.ds(me, 1)] = total[None]
    for j in range(1, mates):
        piece(near_half * mates + lax.rem(me + j, mates)).start()
    for r in range(1, groups):
        landed(lax.rem(me + r, groups)).wait_recv()
    total = rs[0]
    for g in range(1, groups):
        total = total + rs[g]
    total = total * scale
    out[0, 0] = total[:, :bands]
    out[0, 1] = total[:, bands:]

    def drain(c, carry):
        for r in range(groups):
            forward(c, r).wait_send()
        for r in range(1, groups):
            exchange(c, r).wait_send()
        return carry

    lax.fori_loop(0, CHUNKS, drain, 0)
    for r in range(1, groups):
        landed(lax.rem(me + r, groups)).wait_send()


def in_one_kernel(coefficients, stick_count, dest_device, dest_slot, source_stick):
    groups = lax.axis_size("ga")
    _, slots, _, bands, waves = coefficients.shape
    depth = 2 * waves // groups
    sticks = groups * slots
    rows = bands // groups
    scale = (2 * sticks * waves) ** (-0.5)
    any_space = pl.BlockSpec(memory_space=pl.ANY)
    sems = pltpu.SemaphoreType.DMA
    grid_sems = sems((CHUNKS, groups))
    return pl.pallas_call(
        functools.partial(kernel, scale),
        out_shape=jax.ShapeDtypeStruct((1, 2, rows, bands), jnp.float32),
        in_specs=[any_space, pl.BlockSpec(memory_space=pltpu.SMEM), pl.BlockSpec(memory_space=pltpu.VMEM)],
        out_specs=pl.BlockSpec(memory_space=pltpu.VMEM),
        scratch_shapes=[
            pltpu.VMEM((slots, 2, bands, waves), coefficients.dtype),
            pltpu.VMEM((groups, slots, depth, bands), coefficients.dtype),
            pltpu.VMEM((sticks, depth, bands), coefficients.dtype),
            pltpu.VMEM((sticks, depth, bands), coefficients.dtype),
            pltpu.VMEM((sticks * depth, 2 * bands), coefficients.dtype),
            pltpu.VMEM((bands, 2 * bands), jnp.float32),
            pltpu.VMEM((groups, rows, 2 * bands), jnp.float32),
            pltpu.VMEM((groups, 1, slots), jnp.int32),
            pltpu.VMEM((groups, 1, slots), jnp.int32),
            pltpu.SMEM((groups, 1, slots), jnp.int32),
            sems((CHUNKS,)), sems((CHUNKS,)),
            grid_sems, grid_sems, grid_sems, grid_sems,
            sems((groups,)), sems((groups,)), sems, sems, sems,
            sems((groups,)), sems((groups,)),
        ],
        compiler_params=pltpu.CompilerParams(collective_id=0, has_side_effects=True, vmem_limit_bytes=60 * 1024 * 1024),
    )(coefficients, stick_count, source_stick)


def passed_along(value, axis, steps):
    count = lax.axis_size(axis)
    pairs = [(source, (source + steps) % count) for source in range(count)]
    return lax.ppermute(value, axis, pairs)


def with_collectives(coefficients, stick_count, dest_device, dest_slot, source_stick):
    groups = lax.axis_size("ga")
    slot_count = coefficients.shape[1]
    bands = coefficients.shape[3]
    plane_waves = coefficients.shape[4]
    width = plane_waves // groups
    sticks = groups * slot_count
    norm_scale = (2 * groups * slot_count * plane_waves) ** (-0.5)
    split = coefficients[0].reshape(slot_count, 2, bands, groups, width)
    split = split.transpose(3, 0, 1, 4, 2)
    mine = lax.all_to_all(split, "ga", split_axis=0, concat_axis=0, tiled=True)
    mine = mine.reshape(sticks, 2 * width * bands)
    theirs = passed_along(mine, "pool", -1)
    anchor = passed_along(source_stick[0], "pool", -1)
    slot_list = jnp.arange(slot_count, dtype=jnp.int32)
    anchor = jnp.where(slot_list < stick_count[0, 0], anchor, -1)
    anchors = lax.all_gather(anchor, "ga", tiled=True)
    placer = (anchors[:, None] == jnp.arange(sticks, dtype=jnp.int32)[None, :]).astype(jnp.bfloat16)
    ket = jnp.dot(placer, theirs, preferred_element_type=jnp.float32).astype(jnp.bfloat16)
    bra = mine.reshape(sticks, 2, width, bands)
    ket = ket.reshape(sticks, 2, width, bands)
    swapped = jnp.stack([ket[:, 1], -ket[:, 0]], axis=1)
    real_part = jnp.einsum("scgm,scgn->mn", bra, ket, preferred_element_type=jnp.float32)
    imag_part = jnp.einsum("scgm,scgn->mn", bra, swapped, preferred_element_type=jnp.float32)
    partial_value = jnp.stack([real_part, imag_part])
    owned = lax.psum_scatter(partial_value, "ga", scatter_dimension=1, tiled=True)
    return (owned * norm_scale)[None]


def local(coefficients, *rest):
    width = coefficients.shape[4] // lax.axis_size("ga")
    if width % 16 == 0 and coefficients.shape[1] % CHUNKS == 0:
        return in_one_kernel(coefficients, *rest)
    return with_collectives(coefficients, *rest)


def solution(mesh):
    return jax.shard_map(
        local,
        mesh=mesh,
        in_specs=(
            P("pool", "ga", None, None, None),
            P("pool", "ga"),
            P("pool", "ga"),
            P("pool", "ga"),
            P("pool", "ga"),
        ),
        out_specs=P("pool", None, "ga", None),
        check_vma=False,
    )
```

profile of v0, /device:TPU:0, one launch (start us, length us, event | category | flops | bytes accessed | tf_op | source)
XLA Modules:
  0.0 119.6 jit_solution(8395296786277418716)
XLA Ops:
  0.7 117.5 %shard_map.37 = f32[1,2,32,256]{3,2,1,0:T(8,128)} custom-call(bf16[1,32,2,256,128]{4,3,2,1,0:T(8,128)(2,1)} %coef.1, s32[1,1]{1,0:T(1,128)S(6)} %copy.5.count, s32[1,32]{1,0:T(1,128)} %source.1), custom_call_target="tpu_custom_call" | custom-call | tf_op jit(solution)/shard_map/pallas_call | solution.py:256
  118.1 1.5 %copy.6 = f32[1,2,32,256]{3,2,1,0:T(8,128)} copy(f32[1,2,32,256]{3,2,1,0:T(8,128)} %shard_map.37) | data formatting | bytes 131072
where the time goes:
time: 121 us; the launch traced here: 120 us
  Pallas kernels  117 us (97%)
  local copies, waits for them, and re-layouts  1.47 us (1%)
    pallas_call x1, Pallas kernels, in_one_kernel(): pl.pallas_call(functools.partial(kernel, scale), out_shape=jax.ShapeDtype...  117 us

commit v1 on v0

v1 whole, which is shorter than its diff:
```python
import functools

import jax
import jax.numpy as jnp
from jax import lax
from jax.experimental import pallas as pl
from jax.experimental.pallas import tpu as pltpu
from jax.sharding import PartitionSpec as P

MESH = pl.DeviceIdType.MESH
HALVES = 2


def flipped(me, r):
    value = me
    bit = 1
    while bit <= r:
        if r & bit:
            value = value + bit * (1 - 2 * lax.rem(me // bit, 2))
        bit *= 2
    return value


def kernel(
    scale, coef, count, source, out,
    stage, send, mine, theirs_a, theirs_b, ket, acc, rs, near_map, far_map, live_count, slot_map,
    load_sem, own_sem, send_sem, recv_sem, fsend_sem, frecv_sem,
    map_send, map_recv, fmap_send, fmap_recv, map_sem, count_sem, rs_send, rs_recv,
):
    groups, pools = lax.axis_size("ga"), lax.axis_size("pool")
    me, pool = lax.axis_index("ga"), lax.axis_index("pool")
    prev, succ = lax.rem(pool + pools - 1, pools), lax.rem(pool + 1, pools)
    slots, _, bands, waves = stage.shape
    depth = 2 * waves // groups // HALVES
    width = depth // 2
    half = bands // 2
    rows = bands // groups
    lead = slots // 2
    theirs = (theirs_a, theirs_b)
    chunks = [(0, 0, lead), (0, lead, lead), (1, 0, lead), (1, lead, lead // 2), (1, lead + lead // 2, lead // 2)]
    order = [1] + [r for d in range(1, groups // 2) for r in (2 * d + 1, 2 * d)]
    near = [r for r in order if r < groups // 2]
    far = [r for r in order if r >= groups // 2]

    def load(part):
        span = pl.ds(part * lead, lead)
        return pltpu.make_async_copy(coef.at[0, span], stage.at[span], load_sem.at[part])

    def own(c):
        h, first, size = chunks[c]
        return pltpu.make_async_copy(
            send.at[h, me, pl.ds(first, size)],
            mine.at[h, pl.ds(me * slots + first, size)],
            own_sem.at[c],
        )

    def exchange(c, r):
        h, first, size = chunks[c]
        dest = flipped(me, r)
        return pltpu.make_async_remote_copy(
            src_ref=send.at[h, dest, pl.ds(first, size)],
            dst_ref=mine.at[h, pl.ds(me * slots + first, size)],
            send_sem=send_sem.at[c, r],
            recv_sem=recv_sem.at[c, r],
            device_id={"ga": dest},
            device_id_type=MESH,
        )

    def forward(c, r):
        h, first, size = chunks[c]
        span = pl.ds(flipped(me, r) * slots + first, size)
        return pltpu.make_async_remote_copy(
            src_ref=mine.at[h, span],
            dst_ref=theirs[h].at[span],
            send_sem=fsend_sem.at[c, r],
            recv_sem=frecv_sem.at[c, r],
            device_id={"pool": prev},
            device_id_type=MESH,
        )

    def map_copy(r):
        dest = flipped(me, r)
        return pltpu.make_async_remote_copy(
            src_ref=near_map.at[me],
            dst_ref=near_map.at[me],
            send_sem=map_send.at[r],
            recv_sem=map_recv.at[r],
            device_id={"ga": dest},
            device_id_type=MESH,
        )

    def map_forward():
        return pltpu.make_async_remote_copy(
            src_ref=near_map,
            dst_ref=far_map,
            send_sem=fmap_send,
            recv_sem=fmap_recv,
            device_id={"pool": prev},
            device_id_type=MESH,
        )

    own_count = pltpu.make_async_copy(count, live_count, count_sem)
    own_count.start()
    for part in range(2):
        load(part).start()
    own_map = pltpu.make_async_copy(source, near_map.at[me], map_sem)
    own_map.start()

    barrier = pltpu.get_barrier_semaphore()
    for r in order:
        pl.semaphore_signal(barrier, inc=1, device_id={"ga": flipped(me, r)}, device_id_type=MESH)
    for other in (prev, succ):
        pl.semaphore_signal(barrier, inc=1, device_id={"pool": other}, device_id_type=MESH)

    def transposed(part):
        load(part).wait()

        def one(slot, carry):
            live = slot < live_count[0, 0]
            for k in range(2):
                block = stage[slot, k]
                block = jnp.where(live, block, jnp.zeros_like(block)).T
                block = block.reshape(HALVES, groups, width, bands)
                for h in range(HALVES):
                    send[h, :, slot, k * width:(k + 1) * width, :] = block[h]
            return carry

        lax.fori_loop(part * lead, (part + 1) * lead, one, 0)

    own_count.wait()
    transposed(0)
    own_map.wait()
    pl.semaphore_wait(barrier, groups + 1)
    for c in (0, 2):
        for r in near:
            exchange(c, r).start()
    for r in far:
        exchange(0, r).start()
    for r in order:
        map_copy(r).start()
    transposed(1)
    for c in (1, 3, 4):
        for r in near:
            exchange(c, r).start()
    for c in (1, 2, 3, 4):
        for r in far:
            exchange(c, r).start()
    for c in range(len(chunks)):
        own(c).start()
    for c in range(len(chunks)):
        own(c).wait()
        forward(c, 0).start()
    acc[...] = jnp.zeros_like(acc)

    def pass_on(c, steps):
        for r in steps:
            exchange(c, r).wait_recv()
            forward(c, r).start()

    for c in (0, 2, 1, 3, 4):
        pass_on(c, near)
    for r in order:
        map_copy(r).wait()
    map_forward().start()
    for c in (0, 1):
        pass_on(c, far)
    map_forward().wait()
    to_scalar = pltpu.make_async_copy(far_map, slot_map, map_sem)
    to_scalar.start()
    to_scalar.wait()

    def gather(h, b):
        for s in range(slots):
            index = slot_map[b, 0, s]
            block = theirs[h][jnp.maximum(index, 0)]
            block = jnp.where(index >= 0, block, jnp.zeros_like(block))
            span = pl.ds((b * slots + s) * depth, depth)
            ket[span, 0:bands] = block
            ket[span, bands:2 * bands] = jnp.concatenate([block[width:], -block[:width]], axis=0)

    def product(h, b, first, size):
        bra = mine[h, pl.ds(b * slots, slots), :, pl.ds(first, size)].reshape(slots * depth, size)
        other = ket[pl.ds(b * slots * depth, slots * depth), :]
        value = lax.dot_general(
            bra, other, (((0,), (0,)), ((), ())), preferred_element_type=jnp.float32
        )
        acc[pl.ds(first, size), :] += value

    def arrived(cs):
        for c in cs:
            for r in range(groups):
                forward(c, r).wait_recv()

    pass_on(2, far)
    arrived((0, 1))

    def first_half(b, carry):
        gather(0, b)
        product(0, b, 0, bands)
        return carry

    lax.fori_loop(0, groups, first_half, 0)
    for c in (3, 4):
        pass_on(c, far)
    arrived((2, 3, 4))

    near_half = me // (groups // 2)
    far_half = 1 - near_half
    far_first = pl.multiple_of(far_half * half, half)
    near_first = pl.multiple_of(near_half * half, half)

    def far_step(b, carry):
        gather(1, b)
        product(1, b, far_first, half)
        return carry

    lax.fori_loop(0, groups, far_step, 0)

    def piece(dest):
        return pltpu.make_async_remote_copy(
            src_ref=acc.at[pl.ds(dest * rows, rows)],
            dst_ref=rs.at[me],
            send_sem=rs_send.at[dest],
            recv_sem=rs_recv.at[me],
            device_id={"ga": dest},
            device_id_type=MESH,
        )

    def landed(origin):
        return pltpu.make_async_remote_copy(
            src_ref=acc.at[pl.ds(origin * rows, rows)],
            dst_ref=rs.at[origin],
            send_sem=rs_send.at[origin],
            recv_sem=rs_recv.at[origin],
            device_id={"ga": origin},
            device_id_type=MESH,
        )

    product(1, 0, near_first, half)
    mates = groups // 2
    for j in range(mates):
        piece(far_half * mates + lax.rem(me + j, mates)).start()

    def near_step(b, carry):
        product(1, b, near_first, half)
        return carry

    lax.fori_loop(1, groups, near_step, 0)
    total = acc[pl.ds(me * rows, rows), :]
    rs[pl.ds(me, 1)] = total[None]
    for j in range(1, mates):
        piece(near_half * mates + lax.rem(me + j, mates)).start()
    for r in range(1, groups):
        landed(lax.rem(me + r, groups)).wait_recv()
    total = rs[0]
    for g in range(1, groups):
        total = total + rs[g]
    total = total * scale
    out[0, 0] = total[:, :bands]
    out[0, 1] = total[:, bands:]

    for c in range(len(chunks)):
        for r in range(groups):
            forward(c, r).wait_send()
        for r in order:
            exchange(c, r).wait_send()
    for r in range(1, groups):
        landed(lax.rem(me + r, groups)).wait_send()


def in_one_kernel(coefficients, stick_count, dest_device, dest_slot, source_stick):
    groups = lax.axis_size("ga")
    _, slots, _, bands, waves = coefficients.shape
    depth = 2 * waves // groups // HALVES
    sticks = groups * slots
    rows = bands // groups
    scale = (2 * sticks * waves) ** (-0.5)
    any_space = pl.BlockSpec(memory_space=pl.ANY)
    sems = pltpu.SemaphoreType.DMA
    grid_sems = sems((5, groups))
    return pl.pallas_call(
        functools.partial(kernel, scale),
        out_shape=jax.ShapeDtypeStruct((1, 2, rows, bands), jnp.float32),
        in_specs=[any_space, any_space, any_space],
        out_specs=pl.BlockSpec(memory_space=pltpu.VMEM),
        scratch_shapes=[
            pltpu.VMEM((slots, 2, bands, waves), coefficients.dtype),
            pltpu.VMEM((HALVES, groups, slots, depth, bands), coefficients.dtype),
            pltpu.VMEM((HALVES, sticks, depth, bands), coefficients.dtype),
            pltpu.VMEM((sticks, depth, bands), coefficients.dtype),
            pltpu.VMEM((sticks, depth, bands), coefficients.dtype),
            pltpu.VMEM((sticks * depth, 2 * bands), coefficients.dtype),
            pltpu.VMEM((bands, 2 * bands), jnp.float32),
            pltpu.VMEM((groups, rows, 2 * bands), jnp.float32),
            pltpu.VMEM((groups, 1, slots), jnp.int32),
            pltpu.VMEM((groups, 1, slots), jnp.int32),
            pltpu.SMEM((1, 1), jnp.int32),
            pltpu.SMEM((groups, 1, slots), jnp.int32),
            sems((2,)), sems((5,)),
            grid_sems, grid_sems, grid_sems, grid_sems,
            sems((groups,)), sems((groups,)), sems, sems, sems, sems,
            sems((groups,)), sems((groups,)),
        ],
        compiler_params=pltpu.CompilerParams(collective_id=0, has_side_effects=True, vmem_limit_bytes=60 * 1024 * 1024),
    )(coefficients, stick_count, source_stick)


def passed_along(value, axis, steps):
    count = lax.axis_size(axis)
    pairs = [(source, (source + steps) % count) for source in range(count)]
    return lax.ppermute(value, axis, pairs)


def with_collectives(coefficients, stick_count, dest_device, dest_slot, source_stick):
    groups = lax.axis_size("ga")
    slot_count = coefficients.shape[1]
    bands = coefficients.shape[3]
    plane_waves = coefficients.shape[4]
    width = plane_waves // groups
    sticks = groups * slot_count
    norm_scale = (2 * groups * slot_count * plane_waves) ** (-0.5)
    split = coefficients[0].reshape(slot_count, 2, bands, groups, width)
    split = split.transpose(3, 0, 1, 4, 2)
    mine = lax.all_to_all(split, "ga", split_axis=0, concat_axis=0, tiled=True)
    mine = mine.reshape(sticks, 2 * width * bands)
    theirs = passed_along(mine, "pool", -1)
    anchor = passed_along(source_stick[0], "pool", -1)
    slot_list = jnp.arange(slot_count, dtype=jnp.int32)
    anchor = jnp.where(slot_list < stick_count[0, 0], anchor, -1)
    anchors = lax.all_gather(anchor, "ga", tiled=True)
    placer = (anchors[:, None] == jnp.arange(sticks, dtype=jnp.int32)[None, :]).astype(jnp.bfloat16)
    ket = jnp.dot(placer, theirs, preferred_element_type=jnp.float32).astype(jnp.bfloat16)
    bra = mine.reshape(sticks, 2, width, bands)
    ket = ket.reshape(sticks, 2, width, bands)
    swapped = jnp.stack([ket[:, 1], -ket[:, 0]], axis=1)
    real_part = jnp.einsum("scgm,scgn->mn", bra, ket, preferred_element_type=jnp.float32)
    imag_part = jnp.einsum("scgm,scgn->mn", bra, swapped, preferred_element_type=jnp.float32)
    partial_value = jnp.stack([real_part, imag_part])
    owned = lax.psum_scatter(partial_value, "ga", scatter_dimension=1, tiled=True)
    return (owned * norm_scale)[None]


def local(coefficients, *rest):
    groups = lax.axis_size("ga")
    width = coefficients.shape[4] // groups
    if width % 16 == 0 and coefficients.shape[1] % 8 == 0 and groups & (groups - 1) == 0:
        return in_one_kernel(coefficients, *rest)
    return with_collectives(coefficients, *rest)


def solution(mesh):
    return jax.shard_map(
        local,
        mesh=mesh,
        in_specs=(
            P("pool", "ga", None, None, None),
            P("pool", "ga"),
            P("pool", "ga"),
            P("pool", "ga"),
            P("pool", "ga"),
        ),
        out_specs=P("pool", None, "ga", None),
        check_vma=False,
    )
```

time: 121 us -> 119 us (0.983)
    pallas_call x1, Pallas kernels: 117 us -> 116 us  [in_one_kernel(): pl.pallas_call(functools.partial(kernel, scale), out_shape=jax.ShapeDtype...]
where the time goes in v1:
time: 119 us; the launch traced here: 118 us
  Pallas kernels  116 us (97%)
  local copies, waits for them, and re-layouts  1.47 us (1%)
    pallas_call x1, Pallas kernels, in_one_kernel(): pl.pallas_call(functools.partial(kernel, scale), out_shape=jax.ShapeDtype...  116 us

profile of v1, /device:TPU:0, one launch (start us, length us, event | category | flops | bytes accessed | tf_op | source)
XLA Modules:
  0.0 117.9 jit_solution(8573976719194745277)
XLA Ops:
  0.7 115.8 %shard_map.37 = f32[1,2,32,256]{3,2,1,0:T(8,128)} custom-call(bf16[1,32,2,256,128]{4,3,2,1,0:T(8,128)(2,1)} %coef.1, s32[1,1]{1,0:T(1,128)S(6)} %copy.5.count, s32[1,32]{1,0:T(1,128)} %source.1), custom_call_target="tpu_custom_call" | custom-call | tf_op jit(solution)/shard_map/pallas_call | solution.py:281
  116.4 1.5 %copy.6 = f32[1,2,32,256]{3,2,1,0:T(8,128)} copy(f32[1,2,32,256]{3,2,1,0:T(8,128)} %shard_map.37) | data formatting | bytes 131072

commit v2 on v1

--- a/solution.py
+++ b/solution.py
@@ -23,9 +23,9 @@
 
 def kernel(
     scale, coef, count, source, out,
-    stage, send, mine, theirs_a, theirs_b, ket, acc, rs, near_map, far_map, live_count, slot_map,
+    stage, send, mine, theirs_a, theirs_b, ket, acc, rs, leaving, entered, near_map, far_map, live_count, slot_map,
     load_sem, own_sem, send_sem, recv_sem, fsend_sem, frecv_sem,
-    map_send, map_recv, fmap_send, fmap_recv, map_sem, count_sem, rs_send, rs_recv,
+    map_send, map_recv, fmap_send, fmap_recv, map_sem, count_sem, rs_send, rs_recv, cross_send, cross_recv, gate,
 ):
     groups, pools = lax.axis_size("ga"), lax.axis_size("pool")
     me, pool = lax.axis_index("ga"), lax.axis_index("pool")
@@ -42,6 +42,10 @@
     near = [r for r in order if r < groups // 2]
     far = [r for r in order if r >= groups // 2]
 
+    late = [c for c in range(len(chunks)) if chunks[c][0] > 0]
+    second = lax.rem(pool, 2) == 1
+    first = lax.rem(pool, 2) == 0
+
     def load(part):
         span = pl.ds(part * lead, lead)
         return pltpu.make_async_copy(coef.at[0, span], stage.at[span], load_sem.at[part])
@@ -142,9 +146,15 @@
     for c in (1, 3, 4):
         for r in near:
             exchange(c, r).start()
-    for c in (1, 2, 3, 4):
-        for r in far:
-            exchange(c, r).start()
+    for r in far:
+        exchange(1, r).start()
+
+    def late_sends():
+        for c in late:
+            for r in far:
+                exchange(c, r).start()
+
+    pl.when(first)(late_sends)
     for c in range(len(chunks)):
         own(c).start()
     for c in range(len(chunks)):
@@ -191,7 +201,20 @@
             for r in range(groups):
                 forward(c, r).wait_recv()
 
+    @pl.when(second)
+    def _():
+        pl.semaphore_wait(gate, 1)
+        late_sends()
+
     pass_on(2, far)
+
+    @pl.when(first)
+    def _():
+        for c in (0, 1, 2):
+            for r in far:
+                exchange(c, r).wait_send()
+        pl.semaphore_signal(gate, inc=1, device_id={"pool": succ}, device_id_type=MESH)
+
     arrived((0, 1))
 
     def first_half(b, carry):
@@ -216,56 +239,87 @@
 
     lax.fori_loop(0, groups, far_step, 0)
 
-    def piece(dest):
-        return pltpu.make_async_remote_copy(
-            src_ref=acc.at[pl.ds(dest * rows, rows)],
-            dst_ref=rs.at[me],
-            send_sem=rs_send.at[dest],
-            recv_sem=rs_recv.at[me],
+    mates = groups // 2
+    base = near_half * mates
+    seat = me - base
+    across = lax.rem(me + mates, groups)
+
+    def partial_sum(side, part, j, outgoing):
+        dest = base + lax.rem(seat + (j if outgoing else mates - j), mates)
+        block = lax.rem(dest + side * mates, groups)
+        columns = pl.ds(part * bands, bands)
+        return pltpu.make_async_remote_copy(
+            src_ref=acc.at[pl.ds(block * rows, rows), columns],
+            dst_ref=rs.at[side, j, :, columns],
+            send_sem=rs_send.at[side, part, j],
+            recv_sem=rs_recv.at[side, part, j],
             device_id={"ga": dest},
             device_id_type=MESH,
         )
 
-    def landed(origin):
-        return pltpu.make_async_remote_copy(
-            src_ref=acc.at[pl.ds(origin * rows, rows)],
-            dst_ref=rs.at[origin],
-            send_sem=rs_send.at[origin],
-            recv_sem=rs_recv.at[origin],
-            device_id={"ga": origin},
-            device_id_type=MESH,
-        )
-
-    product(1, 0, near_first, half)
-    mates = groups // 2
-    for j in range(mates):
-        piece(far_half * mates + lax.rem(me + j, mates)).start()
+    def crossing(part):
+        columns = pl.ds(part * bands, bands)
+        return pltpu.make_async_remote_copy(
+            src_ref=leaving.at[:, columns],
+            dst_ref=entered.at[:, columns],
+            send_sem=cross_send.at[part],
+            recv_sem=cross_recv.at[part],
+            device_id={"ga": across},
+            device_id_type=MESH,
+        )
+
+    def send_partials(side):
+        for part in range(2):
+            for j in range(1, mates):
+                partial_sum(side, part, j, True).start()
+
+    def summed(side, part):
+        columns = pl.ds(part * bands, bands)
+        block = lax.rem(me + side * mates, groups)
+        value = acc[pl.ds(pl.multiple_of(block * rows, rows), rows), columns]
+        for j in range(1, mates):
+            partial_sum(side, part, j, False).wait_recv()
+            value = value + rs[side, j, :, columns]
+        return value
+
+    send_partials(1)
 
     def near_step(b, carry):
         product(1, b, near_first, half)
         return carry
 
-    lax.fori_loop(1, groups, near_step, 0)
-    total = acc[pl.ds(me * rows, rows), :]
-    rs[pl.ds(me, 1)] = total[None]
-    for j in range(1, mates):
-        piece(near_half * mates + lax.rem(me + j, mates)).start()
-    for r in range(1, groups):
-        landed(lax.rem(me + r, groups)).wait_recv()
-    total = rs[0]
-    for g in range(1, groups):
-        total = total + rs[g]
-    total = total * scale
-    out[0, 0] = total[:, :bands]
-    out[0, 1] = total[:, bands:]
+    lax.fori_loop(0, groups, near_step, 0)
+    send_partials(0)
+    for part in range(2):
+        leaving[:, pl.ds(part * bands, bands)] = summed(1, part)
+        crossing(part).start()
+    for part in range(2):
+        value = summed(0, part)
+        crossing(part).wait_recv()
+        value = value + entered[:, pl.ds(part * bands, bands)]
+        out[0, part] = value * scale
 
     for c in range(len(chunks)):
         for r in range(groups):
             forward(c, r).wait_send()
-        for r in order:
+        for r in near:
             exchange(c, r).wait_send()
-    for r in range(1, groups):
-        landed(lax.rem(me + r, groups)).wait_send()
+    for c in (3, 4):
+        for r in far:
+            exchange(c, r).wait_send()
+
+    @pl.when(second)
+    def _():
+        for c in (0, 1, 2):
+            for r in far:
+                exchange(c, r).wait_send()
+
+    for side in range(2):
+        for part in range(2):
+            for j in range(1, mates):
+                partial_sum(side, part, j, True).wait_send()
+    for part in range(2):
+        crossing(part).wait_send()
 
 
 def in_one_kernel(coefficients, stick_count, dest_device, dest_slot, source_stick):
@@ -291,7 +345,9 @@
             pltpu.VMEM((sticks, depth, bands), coefficients.dtype),
             pltpu.VMEM((sticks * depth, 2 * bands), coefficients.dtype),
             pltpu.VMEM((bands, 2 * bands), jnp.float32),
-            pltpu.VMEM((groups, rows, 2 * bands), jnp.float32),
+            pltpu.VMEM((2, groups // 2, rows, 2 * bands), jnp.float32),
+            pltpu.VMEM((rows, 2 * bands), jnp.float32),
+            pltpu.VMEM((rows, 2 * bands), jnp.float32),
             pltpu.VMEM((groups, 1, slots), jnp.int32),
             pltpu.VMEM((groups, 1, slots), jnp.int32),
             pltpu.SMEM((1, 1), jnp.int32),
@@ -299,7 +355,7 @@
             sems((2,)), sems((5,)),
             grid_sems, grid_sems, grid_sems, grid_sems,
             sems((groups,)), sems((groups,)), sems, sems, sems, sems,
-            sems((groups,)), sems((groups,)),
+            sems((2, 2, groups // 2)), sems((2, 2, groups // 2)), sems((2,)), sems((2,)), pltpu.SemaphoreType.REGULAR,
         ],
         compiler_params=pltpu.CompilerParams(collective_id=0, has_side_effects=True, vmem_limit_bytes=60 * 1024 * 1024),
     )(coefficients, stick_count, source_stick)
@@ -343,7 +399,7 @@
 def local(coefficients, *rest):
     groups = lax.axis_size("ga")
     width = coefficients.shape[4] // groups
-    if width % 16 == 0 and coefficients.shape[1] % 8 == 0 and groups & (groups - 1) == 0:
+    if width % 16 == 0 and coefficients.shape[1] % 8 == 0 and groups & (groups - 1) == 0 and lax.axis_size("pool") % 2 == 0:
         return in_one_kernel(coefficients, *rest)
     return with_collectives(coefficients, *rest)
 

time: 119 us -> 115 us (0.966); the launches traced: 118 us -> 115 us
  Pallas kernels: 116 us -> 113 us
    pallas_call x1, Pallas kernels: 116 us -> 113 us  [in_one_kernel(): pl.pallas_call(functools.partial(kernel, scale), out_shape=jax.ShapeDtype...]
where the time goes in v2:
time: 115 us
  Pallas kernels  113 us (98%)
  local copies, waits for them, and re-layouts  1.47 us (1%)
    pallas_call x1, Pallas kernels, in_one_kernel(): pl.pallas_call(functools.partial(kernel, scale), out_shape=jax.ShapeDtype...  113 us

profile of v2, /device:TPU:0, one launch (start us, length us, event | category | flops | bytes accessed | tf_op | source)
XLA Modules:
  0.0 115.3 jit_solution(10058829296392110484)
XLA Ops:
  0.7 113.2 %shard_map.37 = f32[1,2,32,256]{3,2,1,0:T(8,128)} custom-call(bf16[1,32,2,256,128]{4,3,2,1,0:T(8,128)(2,1)} %coef.1, s32[1,1]{1,0:T(1,128)S(6)} %copy.5.count, s32[1,32]{1,0:T(1,128)} %source.1), custom_call_target="tpu_custom_call" | custom-call | tf_op jit(solution)/shard_map/pallas_call | solution.py:335
  113.8 1.5 %copy.6 = f32[1,2,32,256]{3,2,1,0:T(8,128)} copy(f32[1,2,32,256]{3,2,1,0:T(8,128)} %shard_map.37) | data formatting | bytes 131072

commit v3 on v2

v3 whole, which is shorter than its diff:
```python
import functools

import jax
import jax.numpy as jnp
from jax import lax
from jax.experimental import pallas as pl
from jax.experimental.pallas import tpu as pltpu
from jax.sharding import PartitionSpec as P

MESH = pl.DeviceIdType.MESH
HALVES = 2
CHUNKS = 6


def flipped(me, r):
    value = me
    bit = 1
    while bit <= r:
        if r & bit:
            value = value + bit * (1 - 2 * lax.rem(me // bit, 2))
        bit *= 2
    return value


def kernel(
    scale, coef, count, device, slot, source, out,
    stage, send, mine_a, mine_b, theirs_a, theirs_b, picked, ket, acc, rs, leaving, entered,
    maps, near_map, far_map, live_count, slot_map,
    load_sem, own_sem, send_sem, recv_sem, fsend_sem, frecv_sem,
    map_send, map_recv, fmap_send, fmap_recv, map_sem, count_sem,
    rs_send, rs_recv, cross_send, cross_recv, gate,
):
    groups, pools = lax.axis_size("ga"), lax.axis_size("pool")
    me, pool = lax.axis_index("ga"), lax.axis_index("pool")
    prev, succ = lax.rem(pool + pools - 1, pools), lax.rem(pool + 1, pools)
    slots, _, bands, waves = stage.shape
    depth = 2 * waves // groups // HALVES
    width = depth // 2
    half = bands // 2
    rows = bands // groups
    mine, theirs = (mine_a, mine_b), (theirs_a, theirs_b)
    quarter = slots // 4
    chunks = [
        (0, 0, quarter), (0, quarter, quarter), (0, 2 * quarter, 2 * quarter),
        (1, 0, 2 * quarter), (1, 2 * quarter, quarter), (1, 3 * quarter, quarter),
    ]
    early, late = (0, 1, 2), (3, 4, 5)
    order = [1] + [r for d in range(1, groups // 2) for r in (2 * d + 1, 2 * d)]
    near = [r for r in order if r < groups // 2]
    far = [r for r in order if r >= groups // 2]
    second = lax.rem(pool, 2) == 1
    first = lax.rem(pool, 2) == 0

    def load(part):
        span = pl.ds(part * quarter, quarter)
        return pltpu.make_async_copy(coef.at[0, span], stage.at[span], load_sem.at[part])

    def own(c):
        h, start, size = chunks[c]
        return pltpu.make_async_copy(
            send.at[h, me, pl.ds(start, size)], mine[h].at[me, pl.ds(start, size)], own_sem.at[c]
        )

    def exchange(c, r):
        h, start, size = chunks[c]
        dest = flipped(me, r)
        return pltpu.make_async_remote_copy(
            src_ref=send.at[h, dest, pl.ds(start, size)],
            dst_ref=mine[h].at[me, pl.ds(start, size)],
            send_sem=send_sem.at[c, r],
            recv_sem=recv_sem.at[c, r],
            device_id={"ga": dest},
            device_id_type=MESH,
        )

    def forward(c, r):
        h, start, size = chunks[c]
        origin = flipped(me, r)
        return pltpu.make_async_remote_copy(
            src_ref=mine[h].at[origin, pl.ds(start, size)],
            dst_ref=theirs[h].at[origin, pl.ds(start, size)],
            send_sem=fsend_sem.at[c, r],
            recv_sem=frecv_sem.at[c, r],
            device_id={"pool": prev},
            device_id_type=MESH,
        )

    def map_copy(r):
        dest = flipped(me, r)
        return pltpu.make_async_remote_copy(
            src_ref=near_map.at[me],
            dst_ref=near_map.at[me],
            send_sem=map_send.at[r],
            recv_sem=map_recv.at[r],
            device_id={"ga": dest},
            device_id_type=MESH,
        )

    def map_forward():
        return pltpu.make_async_remote_copy(
            src_ref=near_map,
            dst_ref=far_map,
            send_sem=fmap_send,
            recv_sem=fmap_recv,
            device_id={"pool": prev},
            device_id_type=MESH,
        )

    own_count = pltpu.make_async_copy(count, live_count, count_sem)
    own_count.start()
    for part in range(4):
        load(part).start()
    own_maps = [
        pltpu.make_async_copy(ref, maps.at[n], map_sem.at[n])
        for n, ref in enumerate((device, slot, source))
    ]
    for copy in own_maps:
        copy.start()

    barrier = pltpu.get_barrier_semaphore()
    for r in order:
        pl.semaphore_signal(barrier, inc=1, device_id={"ga": flipped(me, r)}, device_id_type=MESH)
    for other in (prev, succ):
        pl.semaphore_signal(barrier, inc=1, device_id={"pool": other}, device_id_type=MESH)

    def transposed(part):
        load(part).wait()

        def one(place, carry):
            live = place < live_count[0, 0]
            for k in range(2):
                block = stage[place, k]
                block = jnp.where(live, block, jnp.zeros_like(block)).T
                block = block.reshape(HALVES, groups, width, bands)
                for h in range(HALVES):
                    send[h, :, place, k * width:(k + 1) * width, :] = block[h]
            return carry

        lax.fori_loop(part * quarter, (part + 1) * quarter, one, 0)

    def send_off(cs, steps):
        for c in cs:
            for r in steps:
                exchange(c, r).start()

    own_count.wait()
    transposed(0)
    for copy in own_maps:
        copy.wait()
    landing = jnp.where(maps[0] >= 0, maps[0] * slots + maps[1], -1)
    near_map[pl.ds(me, 1)] = jnp.where(second, landing, maps[2])[None]
    pl.semaphore_wait(barrier, groups + 1)
    send_off((0,), near)
    for r in order:
        map_copy(r).start()
    send_off((0,), far)
    transposed(1)
    send_off((1, 3), near)
    send_off((1,), far)
    transposed(2)
    transposed(3)
    send_off((2, 4, 5), near)
    send_off((2,), far)
    pl.when(first)(functools.partial(send_off, late, far))

    for c in range(CHUNKS):
        own(c).start()
    for c in range(CHUNKS):
        own(c).wait()
        forward(c, 0).start()
    acc[...] = jnp.zeros_like(acc)

    def pass_on(c, steps):
        for r in steps:
            exchange(c, r).wait_recv()
            forward(c, r).start()

    def arrived(c):
        for r in range(groups):
            forward(c, r).wait_recv()

    for c in (0, 1, 3, 2, 4, 5):
        pass_on(c, near)
    for r in order:
        map_copy(r).wait()
    map_forward().start()
    for c in early:
        pass_on(c, far)
    map_forward().wait()
    to_scalar = pltpu.make_async_copy(far_map, slot_map, map_sem.at[0])
    to_scalar.start()
    to_scalar.wait()

    @pl.when(first)
    def _():
        pass_on(3, far)
        for c in (0, 1, 2, 3):
            for r in far:
                exchange(c, r).wait_send()
        pl.semaphore_signal(gate, inc=1, device_id={"pool": succ}, device_id_type=MESH)

    @pl.when(second)
    def _():
        pl.semaphore_wait(gate, 1)
        send_off(late, far)

    def looked_up(ref, b, s):
        index = slot_map[b, 0, s]
        place = jnp.maximum(index, 0)
        block = ref[place // slots, lax.rem(place, slots)]
        return jnp.where(index >= 0, block, jnp.zeros_like(block))

    def put_ket(b, s, block):
        ket[b, s, :, 0:bands] = block
        ket[b, s, :, bands:2 * bands] = jnp.concatenate([block[width:], -block[:width]], axis=0)

    def gather_bra(h):
        def step(b, carry):
            for s in range(slots):
                picked[b, s] = looked_up(mine[h], b, s)
            return carry

        lax.fori_loop(0, groups, step, 0)

    def gather_ket(h):
        def step(b, carry):
            for s in range(slots):
                put_ket(b, s, looked_up(theirs[h], b, s))
            return carry

        lax.fori_loop(0, groups, step, 0)

    def plain_ket(c):
        h, start, size = chunks[c]

        def step(b, carry):
            for s in range(start, start + size):
                put_ket(b, s, theirs[h][b, s])
            return carry

        lax.fori_loop(0, groups, step, 0)

    def product(bra, c, row, many):
        _, start, size = chunks[c]
        span = groups * quarter // 2 // size

        def step(i, carry):
            some = pl.ds(i * span, span)
            left = bra[some, pl.ds(start, size), :, pl.ds(row, many)].reshape(span * size * depth, many)
            right = ket[some, pl.ds(start, size)].reshape(span * size * depth, 2 * bands)
            acc[pl.ds(row, many), :] += lax.dot_general(
                left, right, (((0,), (0,)), ((), ())), preferred_element_type=jnp.float32
            )
            return carry

        lax.fori_loop(0, groups // span, step, 0)

    near_half = me // (groups // 2)
    far_row = pl.multiple_of((1 - near_half) * half, half)
    near_row = pl.multiple_of(near_half * half, half)
    last = late[-1]

    @pl.when(first)
    def _():
        gather_bra(0)
        for c in early:
            arrived(c)
            plain_ket(c)
            product(picked, c, 0, bands)
        for c in late[1:]:
            pass_on(c, far)
        gather_bra(1)
        for c in late[:-1]:
            arrived(c)
            plain_ket(c)
            product(picked, c, 0, bands)
        arrived(last)
        plain_ket(last)
        product(picked, last, far_row, half)

    @pl.when(second)
    def _():
        for c in early:
            arrived(c)
        gather_ket(0)
        for c in early:
            product(mine[0], c, 0, bands)
        pass_on(late[0], far)
        for c in late:
            arrived(c)
        gather_ket(1)
        product(mine[1], late[0], 0, bands)
        pass_on(late[1], far)
        product(mine[1], late[1], 0, bands)
        pass_on(last, far)
        product(mine[1], last, far_row, half)

    mates = groups // 2
    base = near_half * mates
    seat = me - base
    across = lax.rem(me + mates, groups)

    def partial_sum(side, part, j, outgoing):
        dest = base + lax.rem(seat + (j if outgoing else mates - j), mates)
        block = lax.rem(dest + side * mates, groups)
        columns = pl.ds(part * bands, bands)
        return pltpu.make_async_remote_copy(
            src_ref=acc.at[pl.ds(block * rows, rows), columns],
            dst_ref=rs.at[side, j, :, columns],
            send_sem=rs_send.at[side, part, j],
            recv_sem=rs_recv.at[side, part, j],
            device_id={"ga": dest},
            device_id_type=MESH,
        )

    def crossing(part):
        columns = pl.ds(part * bands, bands)
        return pltpu.make_async_remote_copy(
            src_ref=leaving.at[:, columns],
            dst_ref=entered.at[:, columns],
            send_sem=cross_send.at[part],
            recv_sem=cross_recv.at[part],
            device_id={"ga": across},
            device_id_type=MESH,
        )

    def send_partials(side):
        for part in range(2):
            for j in range(1, mates):
                partial_sum(side, part, j, True).start()

    def summed(side, part):
        columns = pl.ds(part * bands, bands)
        block = lax.rem(me + side * mates, groups)
        value = acc[pl.ds(pl.multiple_of(block * rows, rows), rows), columns]
        for j in range(1, mates):
            partial_sum(side, part, j, False).wait_recv()
            value = value + rs[side, j, :, columns]
        return value

    send_partials(1)
    pl.when(first)(functools.partial(product, picked, last, near_row, half))
    pl.when(second)(functools.partial(product, mine[1], last, near_row, half))
    send_partials(0)
    for c in range(CHUNKS):
        for r in range(groups):
            forward(c, r).wait_send()
        for r in near:
            exchange(c, r).wait_send()
    for c in late[1:]:
        for r in far:
            exchange(c, r).wait_send()

    @pl.when(second)
    def _():
        for c in (0, 1, 2, 3):
            for r in far:
                exchange(c, r).wait_send()

    for part in range(2):
        leaving[:, pl.ds(part * bands, bands)] = summed(1, part)
        crossing(part).start()
    for part in range(2):
        value = summed(0, part)
        crossing(part).wait_recv()
        value = value + entered[:, pl.ds(part * bands, bands)]
        out[0, part] = value * scale

    for side in range(2):
        for part in range(2):
            for j in range(1, mates):
                partial_sum(side, part, j, True).wait_send()
    for part in range(2):
        crossing(part).wait_send()


def in_one_kernel(coefficients, stick_count, dest_device, dest_slot, source_stick):
    groups = lax.axis_size("ga")
    _, slots, _, bands, waves = coefficients.shape
    depth = 2 * waves // groups // HALVES
    sticks = groups * slots
    rows = bands // groups
    scale = (2 * sticks * waves) ** (-0.5)
    any_space = pl.BlockSpec(memory_space=pl.ANY)
    sems = pltpu.SemaphoreType.DMA
    grid_sems = sems((CHUNKS, groups))
    exchanged = pltpu.VMEM((groups, slots, depth, bands), coefficients.dtype)
    return pl.pallas_call(
        functools.partial(kernel, scale),
        out_shape=jax.ShapeDtypeStruct((1, 2, rows, bands), jnp.float32),
        in_specs=[any_space] * 5,
        out_specs=pl.BlockSpec(memory_space=pltpu.VMEM),
        scratch_shapes=[
            pltpu.VMEM((slots, 2, bands, waves), coefficients.dtype),
            pltpu.VMEM((HALVES, groups, slots, depth, bands), coefficients.dtype),
            exchanged, exchanged, exchanged, exchanged, exchanged,
            pltpu.VMEM((groups, slots, depth, 2 * bands), coefficients.dtype),
            pltpu.VMEM((bands, 2 * bands), jnp.float32),
            pltpu.VMEM((2, groups // 2, rows, 2 * bands), jnp.float32),
            pltpu.VMEM((rows, 2 * bands), jnp.float32),
            pltpu.VMEM((rows, 2 * bands), jnp.float32),
            pltpu.VMEM((3, 1, slots), jnp.int32),
            pltpu.VMEM((groups, 1, slots), jnp.int32),
            pltpu.VMEM((groups, 1, slots), jnp.int32),
            pltpu.SMEM((1, 1), jnp.int32),
            pltpu.SMEM((groups, 1, slots), jnp.int32),
            sems((4,)), sems((CHUNKS,)),
            grid_sems, grid_sems, grid_sems, grid_sems,
            sems((groups,)), sems((groups,)), sems, sems, sems((3,)), sems,
            sems((2, 2, groups // 2)), sems((2, 2, groups // 2)), sems((2,)), sems((2,)), pltpu.SemaphoreType.REGULAR,
        ],
        compiler_params=pltpu.CompilerParams(collective_id=0, has_side_effects=True, vmem_limit_bytes=60 * 1024 * 1024),
    )(coefficients, stick_count, dest_device, dest_slot, source_stick)


def passed_along(value, axis, steps):
    count = lax.axis_size(axis)
    pairs = [(source, (source + steps) % count) for source in range(count)]
    return lax.ppermute(value, axis, pairs)


def with_collectives(coefficients, stick_count, dest_device, dest_slot, source_stick):
    groups = lax.axis_size("ga")
    slot_count = coefficients.shape[1]
    bands = coefficients.shape[3]
    plane_waves = coefficients.shape[4]
    width = plane_waves // groups
    sticks = groups * slot_count
    norm_scale = (2 * groups * slot_count * plane_waves) ** (-0.5)
    split = coefficients[0].reshape(slot_count, 2, bands, groups, width)
    split = split.transpose(3, 0, 1, 4, 2)
    mine = lax.all_to_all(split, "ga", split_axis=0, concat_axis=0, tiled=True)
    mine = mine.reshape(sticks, 2 * width * bands)
    theirs = passed_along(mine, "pool", -1)
    anchor = passed_along(source_stick[0], "pool", -1)
    slot_list = jnp.arange(slot_count, dtype=jnp.int32)
    anchor = jnp.where(slot_list < stick_count[0, 0], anchor, -1)
    anchors = lax.all_gather(anchor, "ga", tiled=True)
    placer = (anchors[:, None] == jnp.arange(sticks, dtype=jnp.int32)[None, :]).astype(jnp.bfloat16)
    ket = jnp.dot(placer, theirs, preferred_element_type=jnp.float32).astype(jnp.bfloat16)
    bra = mine.reshape(sticks, 2, width, bands)
    ket = ket.reshape(sticks, 2, width, bands)
    swapped = jnp.stack([ket[:, 1], -ket[:, 0]], axis=1)
    real_part = jnp.einsum("scgm,scgn->mn", bra, ket, preferred_element_type=jnp.float32)
    imag_part = jnp.einsum("scgm,scgn->mn", bra, swapped, preferred_element_type=jnp.float32)
    partial_value = jnp.stack([real_part, imag_part])
    owned = lax.psum_scatter(partial_value, "ga", scatter_dimension=1, tiled=True)
    return (owned * norm_scale)[None]


def local(coefficients, *rest):
    groups = lax.axis_size("ga")
    width = coefficients.shape[4] // groups
    paired = groups & (groups - 1) == 0 and lax.axis_size("pool") % 2 == 0
    if paired and width % 16 == 0 and coefficients.shape[1] % 8 == 0:
        return in_one_kernel(coefficients, *rest)
    return with_collectives(coefficients, *rest)


def solution(mesh):
    return jax.shard_map(
        local,
        mesh=mesh,
        in_specs=(
            P("pool", "ga", None, None, None),
            P("pool", "ga"),
            P("pool", "ga"),
            P("pool", "ga"),
            P("pool", "ga"),
        ),
        out_specs=P("pool", None, "ga", None),
        check_vma=False,
    )
```

time: 115 us -> 113 us (0.983)
  Pallas kernels: 113 us -> 111 us
    pallas_call x1, Pallas kernels: 113 us -> 111 us  [in_one_kernel(): pl.pallas_call(functools.partial(kernel, scale), out_shape=jax.ShapeDtype...]
where the time goes in v3:
time: 113 us
  Pallas kernels  111 us (98%)
  local copies, waits for them, and re-layouts  1.47 us (1%)
    pallas_call x1, Pallas kernels, in_one_kernel(): pl.pallas_call(functools.partial(kernel, scale), out_shape=jax.ShapeDtype...  111 us

profile of v3, /device:TPU:0, one launch (start us, length us, event | category | flops | bytes accessed | tf_op | source)
XLA Modules:
  0.0 113.1 jit_solution(15944360987658135177)
XLA Ops:
  0.7 111.0 %shard_map.55 = f32[1,2,32,256]{3,2,1,0:T(8,128)} custom-call(bf16[1,32,2,256,128]{4,3,2,1,0:T(8,128)(2,1)} %coef.1, s32[1,1]{1,0:T(1,128)S(6)} %copy.7.count, s32[1,32]{1,0:T(1,128)} %device.1, s32[1,32]{1,0:T(1,128)} %slot.1, s32[1,32]{1,0:T(1,128)} %source.1), custom_call_target="tpu_custom_call" | custom-call | tf_op jit(solution)/shard_map/pallas_call | solution.py:388
  111.6 1.5 %copy.8 = f32[1,2,32,256]{3,2,1,0:T(8,128)} copy(f32[1,2,32,256]{3,2,1,0:T(8,128)} %shard_map.55) | data formatting | bytes 131072

commit v4 on v3

--- a/solution.py
+++ b/solution.py
@@ -55,11 +55,8 @@
         span = pl.ds(part * quarter, quarter)
         return pltpu.make_async_copy(coef.at[0, span], stage.at[span], load_sem.at[part])
 
-    def own(c):
-        h, start, size = chunks[c]
-        return pltpu.make_async_copy(
-            send.at[h, me, pl.ds(start, size)], mine[h].at[me, pl.ds(start, size)], own_sem.at[c]
-        )
+    def own(h):
+        return pltpu.make_async_copy(send.at[h, me], mine[h].at[me], own_sem.at[h])
 
     def exchange(c, r):
         h, start, size = chunks[c]
@@ -67,8 +64,8 @@
         return pltpu.make_async_remote_copy(
             src_ref=send.at[h, dest, pl.ds(start, size)],
             dst_ref=mine[h].at[me, pl.ds(start, size)],
-            send_sem=send_sem.at[c, r],
-            recv_sem=recv_sem.at[c, r],
+            send_sem=send_sem.at[0 if r in near else c + 1],
+            recv_sem=recv_sem.at[c, 0 if r in near else r - len(near)],
             device_id={"ga": dest},
             device_id_type=MESH,
         )
@@ -79,19 +76,43 @@
         return pltpu.make_async_remote_copy(
             src_ref=mine[h].at[origin, pl.ds(start, size)],
             dst_ref=theirs[h].at[origin, pl.ds(start, size)],
-            send_sem=fsend_sem.at[c, r],
-            recv_sem=frecv_sem.at[c, r],
+            send_sem=fsend_sem.at[h],
+            recv_sem=frecv_sem.at[c],
             device_id={"pool": prev},
             device_id_type=MESH,
         )
+
+    def whole(ref, send_one, recv_one, axis, other):
+        return pltpu.make_async_remote_copy(
+            src_ref=ref, dst_ref=ref, send_sem=send_one, recv_sem=recv_one,
+            device_id={axis: other}, device_id_type=MESH,
+        )
+
+    def near_received(c):
+        h, start, size = chunks[c]
+        ref = mine[h].at[pl.ds(0, len(near)), pl.ds(start, size)]
+        whole(ref, send_sem.at[0], recv_sem.at[c, 0], "ga", flipped(me, 1)).wait_recv()
+
+    def near_sent():
+        ref = send.at[:, pl.ds(0, len(near))]
+        whole(ref, send_sem.at[0], recv_sem.at[0, 0], "ga", flipped(me, 1)).wait_send()
+
+    def forwards_sent():
+        for h in range(HALVES):
+            whole(mine[h], fsend_sem.at[h], frecv_sem.at[0], "pool", prev).wait_send()
+
+    def far_sent(c):
+        h, start, size = chunks[c]
+        ref = send.at[h, pl.ds(0, len(far)), pl.ds(start, size)]
+        whole(ref, send_sem.at[c + 1], recv_sem.at[c, 0], "ga", flipped(me, 1)).wait_send()
 
     def map_copy(r):
         dest = flipped(me, r)
         return pltpu.make_async_remote_copy(
             src_ref=near_map.at[me],
             dst_ref=near_map.at[me],
-            send_sem=map_send.at[r],
-            recv_sem=map_recv.at[r],
+            send_sem=map_send,
+            recv_sem=map_recv,
             device_id={"ga": dest},
             device_id_type=MESH,
         )
@@ -111,7 +132,7 @@
     for part in range(4):
         load(part).start()
     own_maps = [
-        pltpu.make_async_copy(ref, maps.at[n], map_sem.at[n])
+        pltpu.make_async_copy(ref, maps.at[n], map_sem)
         for n, ref in enumerate((device, slot, source))
     ]
     for copy in own_maps:
@@ -145,8 +166,7 @@
 
     own_count.wait()
     transposed(0)
-    for copy in own_maps:
-        copy.wait()
+    pltpu.make_async_copy(maps, maps, map_sem).wait()
     landing = jnp.where(maps[0] >= 0, maps[0] * slots + maps[1], -1)
     near_map[pl.ds(me, 1)] = jnp.where(second, landing, maps[2])[None]
     pl.semaphore_wait(barrier, groups + 1)
@@ -163,10 +183,11 @@
     send_off((2,), far)
     pl.when(first)(functools.partial(send_off, late, far))
 
+    for h in range(HALVES):
+        own(h).start()
+    for h in range(HALVES):
+        own(h).wait()
     for c in range(CHUNKS):
-        own(c).start()
-    for c in range(CHUNKS):
-        own(c).wait()
         forward(c, 0).start()
     acc[...] = jnp.zeros_like(acc)
 
@@ -176,18 +197,22 @@
             forward(c, r).start()
 
     def arrived(c):
-        for r in range(groups):
-            forward(c, r).wait_recv()
+        h, start, size = chunks[c]
+        ref = theirs[h].at[:, pl.ds(start, size)]
+        whole(ref, fsend_sem.at[h], frecv_sem.at[c], "pool", prev).wait_recv()
 
     for c in (0, 1, 3, 2, 4, 5):
-        pass_on(c, near)
-    for r in order:
-        map_copy(r).wait()
+        near_received(c)
+        for r in near:
+            forward(c, r).start()
+    every_map = whole(near_map.at[pl.ds(0, groups - 1)], map_send, map_recv, "ga", flipped(me, 1))
+    every_map.wait_send()
+    every_map.wait_recv()
     map_forward().start()
     for c in early:
         pass_on(c, far)
     map_forward().wait()
-    to_scalar = pltpu.make_async_copy(far_map, slot_map, map_sem.at[0])
+    to_scalar = pltpu.make_async_copy(far_map, slot_map, map_sem)
     to_scalar.start()
     to_scalar.wait()
 
@@ -195,8 +220,7 @@
     def _():
         pass_on(3, far)
         for c in (0, 1, 2, 3):
-            for r in far:
-                exchange(c, r).wait_send()
+            far_sent(c)
         pl.semaphore_signal(gate, inc=1, device_id={"pool": succ}, device_id_type=MESH)
 
     @pl.when(second)
@@ -300,15 +324,15 @@
     seat = me - base
     across = lax.rem(me + mates, groups)
 
-    def partial_sum(side, part, j, outgoing):
-        dest = base + lax.rem(seat + (j if outgoing else mates - j), mates)
+    def partial_sum(side, part, j):
+        dest = base + lax.rem(seat + j, mates)
         block = lax.rem(dest + side * mates, groups)
         columns = pl.ds(part * bands, bands)
         return pltpu.make_async_remote_copy(
             src_ref=acc.at[pl.ds(block * rows, rows), columns],
             dst_ref=rs.at[side, j, :, columns],
-            send_sem=rs_send.at[side, part, j],
-            recv_sem=rs_recv.at[side, part, j],
+            send_sem=rs_send,
+            recv_sem=rs_recv.at[side, part],
             device_id={"ga": dest},
             device_id_type=MESH,
         )
@@ -318,7 +342,7 @@
         return pltpu.make_async_remote_copy(
             src_ref=leaving.at[:, columns],
             dst_ref=entered.at[:, columns],
-            send_sem=cross_send.at[part],
+            send_sem=cross_send,
             recv_sem=cross_recv.at[part],
             device_id={"ga": across},
             device_id_type=MESH,
@@ -327,14 +351,15 @@
     def send_partials(side):
         for part in range(2):
             for j in range(1, mates):
-                partial_sum(side, part, j, True).start()
+                partial_sum(side, part, j).start()
 
     def summed(side, part):
         columns = pl.ds(part * bands, bands)
         block = lax.rem(me + side * mates, groups)
         value = acc[pl.ds(pl.multiple_of(block * rows, rows), rows), columns]
+        ref = rs.at[side, pl.ds(1, mates - 1), :, columns]
+        whole(ref, rs_send, rs_recv.at[side, part], "ga", across).wait_recv()
         for j in range(1, mates):
-            partial_sum(side, part, j, False).wait_recv()
             value = value + rs[side, j, :, columns]
         return value
 
@@ -342,20 +367,15 @@
     pl.when(first)(functools.partial(product, picked, last, near_row, half))
     pl.when(second)(functools.partial(product, mine[1], last, near_row, half))
     send_partials(0)
-    for c in range(CHUNKS):
-        for r in range(groups):
-            forward(c, r).wait_send()
-        for r in near:
-            exchange(c, r).wait_send()
+    forwards_sent()
+    near_sent()
     for c in late[1:]:
-        for r in far:
-            exchange(c, r).wait_send()
+        far_sent(c)
 
     @pl.when(second)
     def _():
         for c in (0, 1, 2, 3):
-            for r in far:
-                exchange(c, r).wait_send()
+            far_sent(c)
 
     for part in range(2):
         leaving[:, pl.ds(part * bands, bands)] = summed(1, part)
@@ -366,12 +386,8 @@
         value = value + entered[:, pl.ds(part * bands, bands)]
         out[0, part] = value * scale
 
-    for side in range(2):
-        for part in range(2):
-            for j in range(1, mates):
-                partial_sum(side, part, j, True).wait_send()
-    for part in range(2):
-        crossing(part).wait_send()
+    whole(rs.at[:, pl.ds(1, mates - 1)], rs_send, rs_recv.at[0, 0], "ga", across).wait_send()
+    whole(leaving, cross_send, cross_recv.at[0], "ga", across).wait_send()
 
 
 def in_one_kernel(coefficients, stick_count, dest_device, dest_slot, source_stick):
@@ -383,11 +399,10 @@
     scale = (2 * sticks * waves) ** (-0.5)
     any_space = pl.BlockSpec(memory_space=pl.ANY)
     sems = pltpu.SemaphoreType.DMA
-    grid_sems = sems((CHUNKS, groups))
     exchanged = pltpu.VMEM((groups, slots, depth, bands), coefficients.dtype)
     return pl.pallas_call(
         functools.partial(kernel, scale),
-        out_shape=jax.ShapeDtypeStruct((1, 2, rows, bands), jnp.float32),
+        out_shape=pltpu.VMEM((1, 2, rows, bands), jnp.float32),
         in_specs=[any_space] * 5,
         out_specs=pl.BlockSpec(memory_space=pltpu.VMEM),
         scratch_shapes=[
@@ -404,10 +419,10 @@
             pltpu.VMEM((groups, 1, slots), jnp.int32),
             pltpu.SMEM((1, 1), jnp.int32),
             pltpu.SMEM((groups, 1, slots), jnp.int32),
-            sems((4,)), sems((CHUNKS,)),
-            grid_sems, grid_sems, grid_sems, grid_sems,
-            sems((groups,)), sems((groups,)), sems, sems, sems((3,)), sems,
-            sems((2, 2, groups // 2)), sems((2, 2, groups // 2)), sems((2,)), sems((2,)), pltpu.SemaphoreType.REGULAR,
+            sems((4,)), sems((HALVES,)),
+            sems((CHUNKS + 1,)), sems((CHUNKS, groups // 2 + 1)), sems((HALVES,)), sems((CHUNKS,)),
+            sems, sems, sems, sems, sems, sems,
+            sems, sems((2, 2)), sems, sems((2,)), pltpu.SemaphoreType.REGULAR,
         ],
         compiler_params=pltpu.CompilerParams(collective_id=0, has_side_effects=True, vmem_limit_bytes=60 * 1024 * 1024),
     )(coefficients, stick_count, dest_device, dest_slot, source_stick)

time: 113 us -> 110 us (0.973)
  Pallas kernels: 111 us -> 109 us
    pallas_call x1, Pallas kernels: 111 us -> 109 us  [in_one_kernel(): pl.pallas_call(functools.partial(kernel, scale), out_shape=pltpu.VMEM((1,...]
where the time goes in v4:
time: 110 us
  Pallas kernels  109 us (99%)
    pallas_call x1, Pallas kernels, in_one_kernel(): pl.pallas_call(functools.partial(kernel, scale), out_shape=pltpu.VMEM((1,...  109 us

profile of v4, /device:TPU:0, one launch (start us, length us, event | category | flops | bytes accessed | tf_op | source)
XLA Modules:
  0.0 109.9 jit_solution(13003339012417686150)
XLA Ops:
  0.7 108.6 %shard_map.55 = f32[1,2,32,256]{3,2,1,0:T(8,128)S(1)} custom-call(bf16[1,32,2,256,128]{4,3,2,1,0:T(8,128)(2,1)} %coef.1, s32[1,1]{1,0:T(1,128)S(6)} %copy.8.count, s32[1,32]{1,0:T(1,128)} %device.1, s32[1,32]{1,0:T(1,128)} %slot.1, s32[1,32]{1,0:T(1,128)} %source.1), custom_call_target="tpu_custom_call" | custom-call | tf_op jit(solution)/shard_map/pallas_call | solution.py:403
  109.3 0.6 copy.7

commit v5 on v4

--- a/solution.py
+++ b/solution.py
@@ -9,7 +9,7 @@
 
 MESH = pl.DeviceIdType.MESH
 HALVES = 2
-CHUNKS = 6
+CHUNKS = 5
 
 
 def flipped(me, r):
@@ -42,9 +42,9 @@
     quarter = slots // 4
     chunks = [
         (0, 0, quarter), (0, quarter, quarter), (0, 2 * quarter, 2 * quarter),
-        (1, 0, 2 * quarter), (1, 2 * quarter, quarter), (1, 3 * quarter, quarter),
+        (1, 0, 16), (1, 16, 16),
     ]
-    early, late = (0, 1, 2), (3, 4, 5)
+    early, late = (0, 1, 2), (3, 4)
     order = [1] + [r for d in range(1, groups // 2) for r in (2 * d + 1, 2 * d)]
     near = [r for r in order if r < groups // 2]
     far = [r for r in order if r >= groups // 2]
@@ -179,7 +179,7 @@
     send_off((1,), far)
     transposed(2)
     transposed(3)
-    send_off((2, 4, 5), near)
+    send_off((2, 4), near)
     send_off((2,), far)
     pl.when(first)(functools.partial(send_off, late, far))
 
@@ -187,6 +187,7 @@
         own(h).start()
     for h in range(HALVES):
         own(h).wait()
+
     for c in range(CHUNKS):
         forward(c, 0).start()
     acc[...] = jnp.zeros_like(acc)
@@ -201,7 +202,7 @@
         ref = theirs[h].at[:, pl.ds(start, size)]
         whole(ref, fsend_sem.at[h], frecv_sem.at[c], "pool", prev).wait_recv()
 
-    for c in (0, 1, 3, 2, 4, 5):
+    for c in (0, 1, 3, 2, 4):
         near_received(c)
         for r in near:
             forward(c, r).start()
@@ -266,7 +267,7 @@
 
     def product(bra, c, row, many):
         _, start, size = chunks[c]
-        span = groups * quarter // 2 // size
+        span = groups if many < bands else groups * quarter // 2 // size
 
         def step(i, carry):
             some = pl.ds(i * span, span)
@@ -282,7 +283,6 @@
     near_half = me // (groups // 2)
     far_row = pl.multiple_of((1 - near_half) * half, half)
     near_row = pl.multiple_of(near_half * half, half)
-    last = late[-1]
 
     @pl.when(first)
     def _():
@@ -294,13 +294,10 @@
         for c in late[1:]:
             pass_on(c, far)
         gather_bra(1)
-        for c in late[:-1]:
+        for c in late:
             arrived(c)
             plain_ket(c)
-            product(picked, c, 0, bands)
-        arrived(last)
-        plain_ket(last)
-        product(picked, last, far_row, half)
+            product(picked, c, far_row, half)
 
     @pl.when(second)
     def _():
@@ -313,11 +310,10 @@
         for c in late:
             arrived(c)
         gather_ket(1)
-        product(mine[1], late[0], 0, bands)
-        pass_on(late[1], far)
-        product(mine[1], late[1], 0, bands)
-        pass_on(last, far)
-        product(mine[1], last, far_row, half)
+        for c in late[1:]:
+            pass_on(c, far)
+        for c in late:
+            product(mine[1], c, far_row, half)
 
     mates = groups // 2
     base = near_half * mates
@@ -364,8 +360,13 @@
         return value
 
     send_partials(1)
-    pl.when(first)(functools.partial(product, picked, last, near_row, half))
-    pl.when(second)(functools.partial(product, mine[1], last, near_row, half))
+
+    def near_products(bra):
+        for c in late:
+            product(bra, c, near_row, half)
+
+    pl.when(first)(functools.partial(near_products, picked))
+    pl.when(second)(functools.partial(near_products, mine[1]))
     send_partials(0)
     forwards_sent()
     near_sent()

time: 110 us -> 108 us (0.982)
  Pallas kernels: 109 us -> 107 us
    pallas_call x1, Pallas kernels: 109 us -> 107 us  [in_one_kernel(): pl.pallas_call(functools.partial(kernel, scale), out_shape=pltpu.VMEM((1,...]
where the time goes in v5:
time: 108 us
  Pallas kernels  107 us (99%)
    pallas_call x1, Pallas kernels, in_one_kernel(): pl.pallas_call(functools.partial(kernel, scale), out_shape=pltpu.VMEM((1,...  107 us

profile of v5, /device:TPU:0, one launch (start us, length us, event | category | flops | bytes accessed | tf_op | source)
XLA Modules:
  0.0 108.3 jit_solution(6110451566039271576)
XLA Ops:
  0.7 107.0 %shard_map.55 = f32[1,2,32,256]{3,2,1,0:T(8,128)S(1)} custom-call(bf16[1,32,2,256,128]{4,3,2,1,0:T(8,128)(2,1)} %coef.1, s32[1,1]{1,0:T(1,128)S(6)} %copy.8.count, s32[1,32]{1,0:T(1,128)} %device.1, s32[1,32]{1,0:T(1,128)} %slot.1, s32[1,32]{1,0:T(1,128)} %source.1), custom_call_target="tpu_custom_call" | custom-call | tf_op jit(solution)/shard_map/pallas_call | solution.py:404
  107.7 0.6 copy.7

commit v6 on v5

--- a/solution.py
+++ b/solution.py
@@ -34,7 +34,7 @@
     me, pool = lax.axis_index("ga"), lax.axis_index("pool")
     prev, succ = lax.rem(pool + pools - 1, pools), lax.rem(pool + 1, pools)
     slots, _, bands, waves = stage.shape
-    depth = 2 * waves // groups // HALVES
+    depth = 2 * waves // groups
     width = depth // 2
     half = bands // 2
     rows = bands // groups
@@ -42,7 +42,7 @@
     quarter = slots // 4
     chunks = [
         (0, 0, quarter), (0, quarter, quarter), (0, 2 * quarter, 2 * quarter),
-        (1, 0, 16), (1, 16, 16),
+        (1, 0, 3 * quarter), (1, 3 * quarter, quarter),
     ]
     early, late = (0, 1, 2), (3, 4)
     order = [1] + [r for d in range(1, groups // 2) for r in (2 * d + 1, 2 * d)]
@@ -152,9 +152,9 @@
             for k in range(2):
                 block = stage[place, k]
                 block = jnp.where(live, block, jnp.zeros_like(block)).T
-                block = block.reshape(HALVES, groups, width, bands)
+                block = block.reshape(groups, width, bands)
                 for h in range(HALVES):
-                    send[h, :, place, k * width:(k + 1) * width, :] = block[h]
+                    send[h, :, place, k * width:(k + 1) * width, :] = block[:, :, h * half:(h + 1) * half]
             return carry
 
         lax.fori_loop(part * quarter, (part + 1) * quarter, one, 0)
@@ -175,11 +175,11 @@
         map_copy(r).start()
     send_off((0,), far)
     transposed(1)
-    send_off((1, 3), near)
+    send_off((1,), near)
     send_off((1,), far)
     transposed(2)
     transposed(3)
-    send_off((2, 4), near)
+    send_off((2, 3, 4), near)
     send_off((2,), far)
     pl.when(first)(functools.partial(send_off, late, far))
 
@@ -235,14 +235,14 @@
         block = ref[place // slots, lax.rem(place, slots)]
         return jnp.where(index >= 0, block, jnp.zeros_like(block))
 
-    def put_ket(b, s, block):
-        ket[b, s, :, 0:bands] = block
-        ket[b, s, :, bands:2 * bands] = jnp.concatenate([block[width:], -block[:width]], axis=0)
+    def put_ket(h, b, s, block):
+        ket[b, s, :, h * bands:h * bands + half] = block
+        ket[b, s, :, h * bands + half:(h + 1) * bands] = jnp.concatenate([block[width:], -block[:width]], axis=0)
 
     def gather_bra(h):
         def step(b, carry):
             for s in range(slots):
-                picked[b, s] = looked_up(mine[h], b, s)
+                picked[b, s, :, h * half:(h + 1) * half] = looked_up(mine[h], b, s)
             return carry
 
         lax.fori_loop(0, groups, step, 0)
@@ -250,7 +250,7 @@
     def gather_ket(h):
         def step(b, carry):
             for s in range(slots):
-                put_ket(b, s, looked_up(theirs[h], b, s))
+                put_ket(h, b, s, looked_up(theirs[h], b, s))
             return carry
 
         lax.fori_loop(0, groups, step, 0)
@@ -260,20 +260,19 @@
 
         def step(b, carry):
             for s in range(start, start + size):
-                put_ket(b, s, theirs[h][b, s])
+                put_ket(h, b, s, theirs[h][b, s])
             return carry
 
         lax.fori_loop(0, groups, step, 0)
 
-    def product(bra, c, row, many):
+    def multiply(bra, c, lane, row, many, column, wide, span):
         _, start, size = chunks[c]
-        span = groups if many < bands else groups * quarter // 2 // size
 
         def step(i, carry):
-            some = pl.ds(i * span, span)
-            left = bra[some, pl.ds(start, size), :, pl.ds(row, many)].reshape(span * size * depth, many)
-            right = ket[some, pl.ds(start, size)].reshape(span * size * depth, 2 * bands)
-            acc[pl.ds(row, many), :] += lax.dot_general(
+            some, these = pl.ds(i * span, span), pl.ds(start, size)
+            left = bra[some, these, :, pl.ds(lane, many)].reshape(span * size * depth, many)
+            right = ket[some, these, :, pl.ds(column, wide)].reshape(span * size * depth, wide)
+            acc[pl.ds(row, many), pl.ds(column, wide)] += lax.dot_general(
                 left, right, (((0,), (0,)), ((), ())), preferred_element_type=jnp.float32
             )
             return carry
@@ -281,49 +280,18 @@
         lax.fori_loop(0, groups // span, step, 0)
 
     near_half = me // (groups // 2)
-    far_row = pl.multiple_of((1 - near_half) * half, half)
+    far_half = 1 - near_half
+    far_row = pl.multiple_of(far_half * half, half)
     near_row = pl.multiple_of(near_half * half, half)
-
-    @pl.when(first)
-    def _():
-        gather_bra(0)
-        for c in early:
-            arrived(c)
-            plain_ket(c)
-            product(picked, c, 0, bands)
-        for c in late[1:]:
-            pass_on(c, far)
-        gather_bra(1)
-        for c in late:
-            arrived(c)
-            plain_ket(c)
-            product(picked, c, far_row, half)
-
-    @pl.when(second)
-    def _():
-        for c in early:
-            arrived(c)
-        gather_ket(0)
-        for c in early:
-            product(mine[0], c, 0, bands)
-        pass_on(late[0], far)
-        for c in late:
-            arrived(c)
-        gather_ket(1)
-        for c in late[1:]:
-            pass_on(c, far)
-        for c in late:
-            product(mine[1], c, far_row, half)
 
     mates = groups // 2
     base = near_half * mates
-    seat = me - base
     across = lax.rem(me + mates, groups)
 
     def partial_sum(side, part, j):
-        dest = base + lax.rem(seat + j, mates)
+        dest = flipped(me, j)
         block = lax.rem(dest + side * mates, groups)
-        columns = pl.ds(part * bands, bands)
+        columns = pl.ds(pl.multiple_of(part * bands, bands), bands)
         return pltpu.make_async_remote_copy(
             src_ref=acc.at[pl.ds(block * rows, rows), columns],
             dst_ref=rs.at[side, j, :, columns],
@@ -344,10 +312,9 @@
             device_id_type=MESH,
         )
 
-    def send_partials(side):
-        for part in range(2):
-            for j in range(1, mates):
-                partial_sum(side, part, j).start()
+    def send_partials(side, part):
+        for j in range(mates - 1, 0, -1):
+            partial_sum(side, part, j).start()
 
     def summed(side, part):
         columns = pl.ds(part * bands, bands)
@@ -359,15 +326,66 @@
             value = value + rs[side, j, :, columns]
         return value
 
-    send_partials(1)
-
-    def near_products(bra):
+    def cross(part):
+        leaving[:, pl.ds(part * bands, bands)] = summed(1, part)
+        crossing(part).start()
+
+    low, high = near_half == 0, near_half == 1
+
+    @pl.when(first)
+    def _():
+        gather_bra(0)
+        for c in early:
+            arrived(c)
+            plain_ket(c)
+            multiply(picked, c, 0, 0, half, 0, bands, groups)
+        for c in late[1:]:
+            pass_on(c, far)
+        gather_bra(1)
+        for c in early:
+            multiply(picked, c, half, half, half, 0, bands, groups)
+        send_partials(1, 0)
+        send_partials(0, 0)
         for c in late:
-            product(bra, c, near_row, half)
-
-    pl.when(first)(functools.partial(near_products, picked))
-    pl.when(second)(functools.partial(near_products, mine[1]))
-    send_partials(0)
+            arrived(c)
+            plain_ket(c)
+            multiply(picked, c, far_row, far_row, half, bands, bands, groups)
+        send_partials(1, 1)
+        for c in late:
+            multiply(picked, c, near_row, near_row, half, bands, bands, groups)
+        send_partials(0, 1)
+        cross(0)
+        cross(1)
+
+    @pl.when(second)
+    def _():
+        for c in early:
+            arrived(c)
+        gather_ket(0)
+        for c in early:
+            multiply(mine[0], c, 0, 0, half, 0, bands, groups)
+        for c in late:
+            arrived(c)
+        pass_on(late[0], far)
+        gather_ket(1)
+        for c in early:
+            multiply(mine[0], c, 0, 0, half, bands, bands, groups)
+
+        def send_side(side):
+            for part in range(2):
+                send_partials(side, part)
+
+        pl.when(low)(functools.partial(send_side, 0))
+        pl.when(high)(functools.partial(send_side, 1))
+        for c in late[1:]:
+            pass_on(c, far)
+        for c in late:
+            multiply(mine[1], c, 0, half, half, 0, 2 * bands, groups)
+        pl.when(low)(functools.partial(send_side, 1))
+        pl.when(high)(functools.partial(send_side, 0))
+        cross(0)
+        cross(1)
+
     forwards_sent()
     near_sent()
     for c in late[1:]:
@@ -379,13 +397,11 @@
             far_sent(c)
 
     for part in range(2):
-        leaving[:, pl.ds(part * bands, bands)] = summed(1, part)
-        crossing(part).start()
-    for part in range(2):
         value = summed(0, part)
         crossing(part).wait_recv()
-        value = value + entered[:, pl.ds(part * bands, bands)]
-        out[0, part] = value * scale
+        value = (value + entered[:, pl.ds(part * bands, bands)]) * scale
+        out[0, 0, :, pl.ds(part * half, half)] = value[:, :half]
+        out[0, 1, :, pl.ds(part * half, half)] = value[:, half:]
 
     whole(rs.at[:, pl.ds(1, mates - 1)], rs_send, rs_recv.at[0, 0], "ga", across).wait_send()
     whole(leaving, cross_send, cross_recv.at[0], "ga", across).wait_send()
@@ -394,13 +410,14 @@
 def in_one_kernel(coefficients, stick_count, dest_device, dest_slot, source_stick):
     groups = lax.axis_size("ga")
     _, slots, _, bands, waves = coefficients.shape
-    depth = 2 * waves // groups // HALVES
+    depth = 2 * waves // groups
+    half = bands // HALVES
     sticks = groups * slots
     rows = bands // groups
     scale = (2 * sticks * waves) ** (-0.5)
     any_space = pl.BlockSpec(memory_space=pl.ANY)
     sems = pltpu.SemaphoreType.DMA
-    exchanged = pltpu.VMEM((groups, slots, depth, bands), coefficients.dtype)
+    exchanged = pltpu.VMEM((groups, slots, depth, half), coefficients.dtype)
     return pl.pallas_call(
         functools.partial(kernel, scale),
         out_shape=pltpu.VMEM((1, 2, rows, bands), jnp.float32),
@@ -408,8 +425,9 @@
         out_specs=pl.BlockSpec(memory_space=pltpu.VMEM),
         scratch_shapes=[
             pltpu.VMEM((slots, 2, bands, waves), coefficients.dtype),
-            pltpu.VMEM((HALVES, groups, slots, depth, bands), coefficients.dtype),
-            exchanged, exchanged, exchanged, exchanged, exchanged,
+            pltpu.VMEM((HALVES, groups, slots, depth, half), coefficients.dtype),
+            exchanged, exchanged, exchanged, exchanged,
+            pltpu.VMEM((groups, slots, depth, bands), coefficients.dtype),
             pltpu.VMEM((groups, slots, depth, 2 * bands), coefficients.dtype),
             pltpu.VMEM((bands, 2 * bands), jnp.float32),
             pltpu.VMEM((2, groups // 2, rows, 2 * bands), jnp.float32),
@@ -468,7 +486,7 @@
     groups = lax.axis_size("ga")
     width = coefficients.shape[4] // groups
     paired = groups & (groups - 1) == 0 and lax.axis_size("pool") % 2 == 0
-    if paired and width % 16 == 0 and coefficients.shape[1] % 8 == 0:
+    if paired and width % 16 == 0 and coefficients.shape[1] % 8 == 0 and coefficients.shape[3] % 256 == 0:
         return in_one_kernel(coefficients, *rest)
     return with_collectives(coefficients, *rest)
 

time: 108 us -> 108 us (level)
  no operation moved by 1% of the time
where the time goes in v6:
time: 108 us; the launch traced here: 107 us
  Pallas kernels  106 us (98%)
    pallas_call x1, Pallas kernels, in_one_kernel(): pl.pallas_call(functools.partial(kernel, scale), out_shape=pltpu.VMEM((1,...  106 us

profile of v6, /device:TPU:0, one launch (start us, length us, event | category | flops | bytes accessed | tf_op | source)
XLA Modules:
  0.0 107.4 jit_solution(5200541768543874224)
XLA Ops:
  0.7 106.2 %shard_map.55 = f32[1,2,32,256]{3,2,1,0:T(8,128)S(1)} custom-call(bf16[1,32,2,256,128]{4,3,2,1,0:T(8,128)(2,1)} %coef.1, s32[1,1]{1,0:T(1,128)S(6)} %copy.8.count, s32[1,32]{1,0:T(1,128)} %device.1, s32[1,32]{1,0:T(1,128)} %slot.1, s32[1,32]{1,0:T(1,128)} %source.1), custom_call_target="tpu_custom_call" | custom-call | tf_op jit(solution)/shard_map/pallas_call | solution.py:421
  106.8 0.6 copy.7

commit v7 on v6

--- a/solution.py
+++ b/solution.py
@@ -351,10 +351,10 @@
             plain_ket(c)
             multiply(picked, c, far_row, far_row, half, bands, bands, groups)
         send_partials(1, 1)
+        cross(0)
         for c in late:
             multiply(picked, c, near_row, near_row, half, bands, bands, groups)
         send_partials(0, 1)
-        cross(0)
         cross(1)
 
     @pl.when(second)

time: 108 us -> 108 us (level)
  no operation moved by 1% of the time
where the time goes in v7:
time: 108 us; the launch traced here: 107 us
  Pallas kernels  106 us (98%)
    pallas_call x1, Pallas kernels, in_one_kernel(): pl.pallas_call(functools.partial(kernel, scale), out_shape=pltpu.VMEM((1,...  106 us

profile of v7, /device:TPU:0, one launch (start us, length us, event | category | flops | bytes accessed | tf_op | source)
XLA Modules:
  0.0 107.4 jit_solution(13730825159544139510)
XLA Ops:
  0.7 106.2 %shard_map.55 = f32[1,2,32,256]{3,2,1,0:T(8,128)S(1)} custom-call(bf16[1,32,2,256,128]{4,3,2,1,0:T(8,128)(2,1)} %coef.1, s32[1,1]{1,0:T(1,128)S(6)} %copy.8.count, s32[1,32]{1,0:T(1,128)} %device.1, s32[1,32]{1,0:T(1,128)} %slot.1, s32[1,32]{1,0:T(1,128)} %source.1), custom_call_target="tpu_custom_call" | custom-call | tf_op jit(solution)/shard_map/pallas_call | solution.py:421
  106.8 0.6 copy.7

commit v8 on v7

--- a/solution.py
+++ b/solution.py
@@ -346,13 +346,17 @@
             multiply(picked, c, half, half, half, 0, bands, groups)
         send_partials(1, 0)
         send_partials(0, 0)
-        for c in late:
+        for c in late[:-1]:
+            arrived(c)
+            plain_ket(c)
+            multiply(picked, c, 0, 0, bands, bands, bands, groups)
+        for c in late[-1:]:
             arrived(c)
             plain_ket(c)
             multiply(picked, c, far_row, far_row, half, bands, bands, groups)
         send_partials(1, 1)
         cross(0)
-        for c in late:
+        for c in late[-1:]:
             multiply(picked, c, near_row, near_row, half, bands, bands, groups)
         send_partials(0, 1)
         cross(1)

time: 108 us -> 108 us (level)
  no operation moved by 1% of the time
where the time goes in v8:
time: 108 us; the launch traced here: 107 us
  Pallas kernels  106 us (98%)
    pallas_call x1, Pallas kernels, in_one_kernel(): pl.pallas_call(functools.partial(kernel, scale), out_shape=pltpu.VMEM((1,...  106 us

profile of v8, /device:TPU:0, one launch (start us, length us, event | category | flops | bytes accessed | tf_op | source)
XLA Modules:
  0.0 107.4 jit_solution(11960869811114838349)
XLA Ops:
  0.7 106.2 %shard_map.55 = f32[1,2,32,256]{3,2,1,0:T(8,128)S(1)} custom-call(bf16[1,32,2,256,128]{4,3,2,1,0:T(8,128)(2,1)} %coef.1, s32[1,1]{1,0:T(1,128)S(6)} %copy.8.count, s32[1,32]{1,0:T(1,128)} %device.1, s32[1,32]{1,0:T(1,128)} %slot.1, s32[1,32]{1,0:T(1,128)} %source.1), custom_call_target="tpu_custom_call" | custom-call | tf_op jit(solution)/shard_map/pallas_call | solution.py:425
  106.8 0.6 copy.7
